TPU v7x, 32 devices: a whole 2x2x4 slice. The times are simulated.
32 devices in a mesh: seq: 4 (over z), blk: 4 (over y, core), uly: 2 (over x).
Axes of the slice: x: 2, y: 2, z: 4, core: 2. Of those that a mesh axis runs over, the one named last changes fastest.
Arguments:
- queries: bfloat16 [8192, 5120], P(('seq', 'blk', 'uly')), parts along dimension 0, may hold values from -60 to 60, as said below
- keys: bfloat16 [8192, 1024], P(('seq', 'blk', 'uly')), parts along dimension 0, may hold values from -60 to 60, as said below
- values: bfloat16 [8192, 1024], P(('seq', 'blk', 'uly')), parts along dimension 0, may hold values from -6 to 6
- positions: int32 [3, 8192], P(None, ('seq', 'blk', 'uly')), parts along dimension 1, may hold values from 0 to 526
- doc_lengths: int32 [32], P('seq'), parts along dimension 0, may hold values from 1 to 1024, 2048 in all
Outputs:
- attended: bfloat16 [8192, 5120], P(('seq', 'blk', 'uly')), parts along dimension 0
There are 4 independent parts, one for each index of `seq`. A program takes and returns all parts, laid end to end along the dimension named above; each array names one. Nothing has to cross between parts.
Inputs may be any that keep to these rules, and one draw needn't show every extreme that they name: queries; the query rows hold values of order one, a few rows may be much larger. keys; the key rows hold values of order one, a few rows may be much larger.
All inputs are finite; a program needn't handle non-finite values.
Results may differ from a plain program's by a relative error of at most 0.0055.
Values may be sent and summed in bfloat16 or wider, within the bound.
A program may use at most 384 MiB of HBM per device.

v0:
```python
import functools
import math

import jax
import jax.numpy as jnp
import numpy as np
from jax import lax
from jax.experimental import pallas as pl
from jax.experimental.pallas import tpu as pltpu
from jax.sharding import PartitionSpec as P

HEAD_SIZE = 128
QUERY_PER_KEY = 5
AHEAD = 3
RELAY_AHEAD = 1


def frequencies():
    pair = np.arange(HEAD_SIZE) % (HEAD_SIZE // 2)
    return np.power(1000000.0, -2.0 * pair / HEAD_SIZE).astype(np.float32)[None, :]


def rotary_tables(places, freq):
    rows = places.shape[1]
    half = HEAD_SIZE // 2
    row = lax.broadcasted_iota(jnp.int32, (rows, rows), 0)
    col = lax.broadcasted_iota(jnp.int32, (rows, rows), 1)
    column = [
        jnp.sum(
            jnp.where(row == col, places[p : p + 1, :].astype(jnp.float32), 0.0),
            axis=1,
            keepdims=True,
        )
        for p in range(3)
    ]
    lane = lax.broadcasted_iota(jnp.int32, (rows, HEAD_SIZE), 1)
    upper = lane >= half
    pair = jnp.where(upper, lane - half, lane)
    first = HEAD_SIZE // 8
    second = first + 3 * HEAD_SIZE // 16
    chosen = jnp.where(pair < first, column[0], jnp.where(pair < second, column[1], column[2]))
    angle = chosen * freq
    turns = jnp.floor(angle * (2.0 / math.pi) + 0.5)
    rest = angle - turns * 1.5703125
    rest = rest - turns * 4.8351287841796875e-4
    rest = rest - turns * 3.138552419841289520264e-7
    rest = rest - turns * 6.07710050630396597660e-11
    quarter = turns.astype(jnp.int32) & 3
    square = rest * rest
    sine = rest + rest * square * (
        -1.0 / 6 + square * (1.0 / 120 + square * (-1.0 / 5040 + square * (1.0 / 362880)))
    )
    cosine = 1.0 + square * (
        -0.5 + square * (1.0 / 24 + square * (-1.0 / 720 + square * (1.0 / 40320)))
    )
    swap = (quarter & 1) == 1
    sin_turned = jnp.where(swap, cosine, sine)
    cos_turned = jnp.where(swap, sine, cosine)
    sin_turned = jnp.where(quarter >= 2, -sin_turned, sin_turned)
    cos_turned = jnp.where((quarter == 1) | (quarter == 2), -cos_turned, cos_turned)
    return cos_turned, jnp.where(upper, sin_turned, -sin_turned)


def routes(blocks, lanes):
    count = blocks * lanes
    window = count // 2

    def place(r):
        return (r // lanes // 2, r % lanes), r // lanes % 2

    def member(chip, core):
        return (chip[0] * 2 + core) * lanes + chip[1]

    found = {}
    for s in range(count):
        home, own_core = place(s)
        wanting = set(range(s + 1, min(count, s + window + 1)))

        def entry(chip):
            if chip == home:
                return s
            for core in (own_core, 1 - own_core):
                if member(chip, core) in wanting:
                    return member(chip, core)
            return None

        for half in (0, 1):
            for r in sorted(wanting):
                chip, _ = place(r)
                source = entry(chip)
                if source == r:
                    options = []
                    if chip[1] != home[1]:
                        options.append(entry((chip[0], home[1])))
                    if chip[0] > home[0]:
                        options.append(entry((chip[0] - 1, chip[1])))
                    if half:
                        options.reverse()
                    options = [o for o in options if o is not None] + [s]
                    source = options[0]
                found.setdefault((source - s, r - source), (set(), set()))[half].add(source)
    return sorted(found.items(), key=lambda item: (-item[0][0], item[0][1]))


def among(me, devices):
    hit = jnp.bool_(False)
    for device in sorted(devices):
        hit = hit | (me == device)
    return hit


def kernel(
    plan, lanes, count, window, kheads,
    lengths, places, freq, keys, values, queries, out,
    cosine, sine, kv, qbuf, bias, q_sem, send_sem, recv_sem,
):
    rows = keys.shape[0]
    size = HEAD_SIZE
    group = QUERY_PER_KEY * size
    me = lax.axis_index("blk") * lanes + lax.axis_index("uly")
    fetch = pltpu.make_async_copy(queries, qbuf, q_sem)
    fetch.start()

    def where_is(r):
        return {"blk": lax.div(r, lanes), "uly": lax.rem(r, lanes)}

    def column(h, width):
        return pl.ds(pl.multiple_of(h * width, width), width)

    def fill_ones(i, carry):
        kv[lax.div(i, kheads), lax.rem(i, kheads), :, 2 * size:] = jnp.ones((rows, size), kv.dtype)
        return carry

    lax.fori_loop(0, (window + 1) * kheads, fill_ones, 0)
    for slot in range(1, window + 1):
        @pl.when(me < slot)
        def _():
            def clear(h, carry):
                kv[slot, h, :, : 2 * size] = jnp.zeros((rows, 2 * size), kv.dtype)
                return carry

            lax.fori_loop(0, kheads, clear, 0)

    barrier = pltpu.get_barrier_semaphore()
    for offset in range(1, count):
        peer = lax.rem(me + offset, count)
        pl.semaphore_signal(
            barrier, inc=1, device_id=where_is(peer), device_id_type=pl.DeviceIdType.MESH
        )

    cosine[...], sine[...] = rotary_tables(places, freq[...])

    def turn(x):
        x = x.astype(jnp.float32)
        return (x * cosine[...] + pltpu.roll(x, size // 2, 1) * sine[...]).astype(jnp.bfloat16)

    def own_block(h, carry):
        kv[0, h, :, :size] = turn(keys[:, column(h, size)])
        kv[0, h, :, size : 2 * size] = values[:, column(h, size)]
        return carry

    lax.fori_loop(0, kheads, own_block, 0)
    pl.semaphore_wait(barrier, count - 1)

    def copy_of(index, slot, step, h):
        return pltpu.make_async_remote_copy(
            src_ref=kv.at[slot, h, :, pl.ds(0, 2 * size)],
            dst_ref=kv.at[slot + step, h, :, pl.ds(0, 2 * size)],
            send_sem=send_sem.at[index, h],
            recv_sem=recv_sem.at[slot + step, h],
            device_id=where_is(me + step),
            device_id_type=pl.DeviceIdType.MESH,
        )

    def arrival(slot, h):
        return pltpu.make_async_remote_copy(
            src_ref=kv.at[slot, h, :, pl.ds(0, 2 * size)],
            dst_ref=kv.at[slot, h, :, pl.ds(0, 2 * size)],
            send_sem=send_sem.at[0, h],
            recv_sem=recv_sem.at[slot, h],
            device_id=where_is(me),
            device_id_type=pl.DeviceIdType.MESH,
        )

    def sends(senders, h):
        even, odd = senders
        if even == odd:
            return among(me, even)
        is_even = lax.rem(h, 2) == 0
        return (is_even & among(me, even)) | (jnp.logical_not(is_even) & among(me, odd))

    def send(slot, h):
        for index, ((from_slot, step), senders) in enumerate(plan):
            if from_slot == slot:
                @pl.when(sends(senders, h))
                def _():
                    copy_of(index, slot, step, h).start()

    def relays(slot, h):
        hit = jnp.bool_(False)
        for (from_slot, _), senders in plan:
            if from_slot == slot:
                hit = hit | sends(senders, h)
        return hit

    def first_sends(h, carry):
        send(0, h)
        return carry

    lax.fori_loop(0, AHEAD, first_sends, 0)

    def forward(h, carry):
        for slot in range(window, 0, -1):
            @pl.when(relays(slot, h))
            def _():
                arrival(slot, h).wait_recv()
                send(slot, h)

        return carry

    row = lax.broadcasted_iota(jnp.int32, (rows, rows), 0) + me * rows
    col = lax.broadcasted_iota(jnp.int32, (rows, rows), 1)
    start = jnp.zeros((rows, rows), jnp.int32)
    end = jnp.int32(0)
    for d in range(lengths.shape[0]):
        end = end + lengths[d]
        start = start + jnp.where(row >= end, lengths[d], 0)
    for slot in range(window + 1):
        key = col + (me - slot) * rows
        allowed = (key >= start) & (key <= row)
        bias[:, slot * rows : (slot + 1) * rows] = jnp.where(allowed, 0.0, -1e30)

    fetch.wait()
    lax.fori_loop(0, RELAY_AHEAD, forward, 0)
    scale = math.log2(math.e) / math.sqrt(size)

    def head(h, carry):
        @pl.when(h + AHEAD < kheads)
        def _():
            send(0, h + AHEAD)

        @pl.when(h + RELAY_AHEAD < kheads)
        def _():
            forward(h + RELAY_AHEAD, carry)

        for slot in range(1, window + 1):
            @pl.when((me >= slot) & jnp.logical_not(relays(slot, h)))
            def _():
                arrival(slot, h).wait_recv()

        k_all = kv[:, h, :, :size].reshape((window + 1) * rows, size)
        v_all = kv[:, h, :, size:].reshape((window + 1) * rows, 2 * size)
        for g in range(QUERY_PER_KEY):
            at = pl.ds(pl.multiple_of(h * group + g * size, size), size)
            q = turn(qbuf[:, at])
            scores = lax.dot_general(
                q, k_all, (((1,), (1,)), ((), ())), preferred_element_type=jnp.float32
            )
            scores = scores + bias[...]
            best = jnp.max(scores, axis=1, keepdims=True)
            weights = jnp.exp2((scores - best) * scale).astype(jnp.bfloat16)
            summed = jnp.dot(weights, v_all, preferred_element_type=jnp.float32)
            out[:, at] = (summed[:, :size] / summed[:, size:]).astype(jnp.bfloat16)
        return carry

    lax.fori_loop(0, kheads, head, 0)

    def finish(h, carry):
        for index, ((slot, step), senders) in enumerate(plan):
            @pl.when(sends(senders, h))
            def _():
                copy_of(index, slot, step, h).wait_send()

        return carry

    lax.fori_loop(0, kheads, finish, 0)


def local(blocks, lanes, queries, keys, values, positions, doc_lengths):
    rows = queries.shape[0]
    kheads = keys.shape[1] // HEAD_SIZE
    count = blocks * lanes
    window = count // 2
    plan = routes(blocks, lanes)
    vmem = pl.BlockSpec(memory_space=pltpu.VMEM)
    anywhere = pl.BlockSpec(memory_space=pl.ANY)
    return pl.pallas_call(
        functools.partial(kernel, plan, lanes, count, window, kheads),
        out_shape=pltpu.VMEM(queries.shape, jnp.bfloat16),
        in_specs=[pl.BlockSpec(memory_space=pltpu.SMEM), vmem, vmem, vmem, vmem, anywhere],
        out_specs=vmem,
        scratch_shapes=[
            pltpu.VMEM((rows, HEAD_SIZE), jnp.float32),
            pltpu.VMEM((rows, HEAD_SIZE), jnp.float32),
            pltpu.VMEM((window + 1, kheads, rows, 3 * HEAD_SIZE), jnp.bfloat16),
            pltpu.VMEM(queries.shape, jnp.bfloat16),
            pltpu.VMEM((rows, (window + 1) * rows), jnp.float32),
            pltpu.SemaphoreType.DMA,
            pltpu.SemaphoreType.DMA((len(plan), kheads)),
            pltpu.SemaphoreType.DMA((window + 1, kheads)),
        ],
        compiler_params=pltpu.CompilerParams(
            collective_id=0, has_side_effects=True, vmem_limit_bytes=60 * 1024 * 1024
        ),
        name="windowed_attention",
    )(doc_lengths, positions, jnp.asarray(frequencies()), keys, values, queries)


def solution(mesh):
    in_specs = (
        P(("seq", "blk", "uly"), None),
        P(("seq", "blk", "uly"), None),
        P(("seq", "blk", "uly"), None),
        P(None, ("seq", "blk", "uly")),
        P("seq"),
    )
    out_specs = P(("seq", "blk", "uly"), None)
    body = functools.partial(local, mesh.shape["blk"], mesh.shape["uly"])
    return jax.shard_map(body, mesh=mesh, in_specs=in_specs, out_specs=out_specs, check_vma=False)
```

profile of v0, /device:TPU:12, one launch (start us, length us, event | category | flops | bytes accessed | tf_op | source)
XLA Modules:
  0.0 46.4 jit_solution(13163053316453070483)
XLA Ops:
  0.0 44.9 %windowed_attention.1 = bf16[256,5120]{1,0:T(8,128)(2,1)S(1)} custom-call(s32[8]{0:T(128)} %lengths.1, s32[3,256]{1,0:T(4,128)} %places.1, f32[1,128]{1,0:T(1,128)} %constant.2.clone.freq, bf16[256,1024]{1,0:T(8,128)(2,1)} %keys.1, bf16[256,1024]{1,0:T(8,128)(2,1)} %values.1, bf16[256,5120]{1,0:T(8,128)(2,1)} %queries.1), custom_call_target="tpu_custom_call" | custom-call | tf_op jit(solution)/shard_map/windowed_attention/pallas_call | solution.py:287
  44.9 1.5 %copy.8 = bf16[256,5120]{1,0:T(8,128)(2,1)} copy(bf16[256,5120]{1,0:T(8,128)(2,1)S(1)} %windowed_attention.1) | data formatting | bytes 5242880
where the time goes:
time: 46.9 us; the launch traced here: 46.4 us
  Pallas kernels  44.9 us (96%)
  local copies, waits for them, and re-layouts  1.49 us (3%)
    pallas_call x1, Pallas kernels, local(): pl.pallas_call(functools.partial(kernel, plan, lanes, count, window, khea...  44.9 us
    unnamed x1, local copies, waits for them, and re-layouts  1.49 us

commit v1 on v0

v1 whole, which is shorter than its diff:
```python
import functools
import math

import jax
import jax.numpy as jnp
import numpy as np
from jax import lax
from jax.experimental import pallas as pl
from jax.experimental.pallas import tpu as pltpu
from jax.sharding import PartitionSpec as P

HEAD_SIZE = 128
QUERY_PER_KEY = 5
BURST = 8
SETTLED = 5
FAR = -1e30
SUBLANES = 8


TABLE = {
    "own": {
        1: (8, 4, 2, 0, 8, 8, 2, 0),
        2: (5, 8, 0, 0, 5, 5, 0, 0),
        4: (8, 8, 6, 3, 0, 0, 0, 0),
    },
    "relay": {
        4: ((0, 0, 0, 0, 0, 6, 2, 2), (0, 0, 0, 0, 0, 1, 0, 0)),
        3: ((0, 0, 0, 0, 0, 0, 1, 0), (0, 0, 0, 0, 0, 0, 2, 0)),
        1: ((0, 0, 0, 0, 0, 2, 0, 0), (0, 1, 0, 1, 0, 1, 0, 0)),
    },
    "first": (1, 2, 3, 3, 3, 4, 2, 2),
}


def frequencies():
    pair = np.arange(HEAD_SIZE // 2)
    value = np.power(1000000.0, -2.0 * pair / HEAD_SIZE).astype(np.float32)
    return np.repeat(value[:, None], HEAD_SIZE, axis=1)


def rotary_tables(places, freq):
    rows = places.shape[1]
    half = HEAD_SIZE // 2
    pair = lax.broadcasted_iota(jnp.int32, (half, rows), 0)
    first = HEAD_SIZE // 8
    second = first + 3 * HEAD_SIZE // 16
    place = places.astype(jnp.float32)
    chosen = jnp.where(pair < first, place[0:1], jnp.where(pair < second, place[1:2], place[2:3]))
    angle = chosen * jnp.concatenate([freq] * (rows // HEAD_SIZE), axis=1)
    turns = jnp.floor(angle * (2.0 / math.pi) + 0.5)
    rest = angle - turns * 1.5703125
    rest = rest - turns * 4.8351287841796875e-4
    rest = rest - turns * 3.138552419841289520264e-7
    rest = rest - turns * 6.07710050630396597660e-11
    quarter = turns.astype(jnp.int32) & 3
    square = rest * rest
    sine = rest + rest * square * (
        -1.0 / 6 + square * (1.0 / 120 + square * (-1.0 / 5040 + square * (1.0 / 362880)))
    )
    cosine = 1.0 + square * (
        -0.5 + square * (1.0 / 24 + square * (-1.0 / 720 + square * (1.0 / 40320)))
    )
    swap = (quarter & 1) == 1
    sin_turned = jnp.where(swap, cosine, sine)
    cos_turned = jnp.where(swap, sine, cosine)
    sin_turned = jnp.where(quarter >= 2, -sin_turned, sin_turned)
    cos_turned = jnp.where((quarter == 1) | (quarter == 2), -cos_turned, cos_turned)
    return cos_turned, sin_turned


def routes(blocks, lanes):
    count = blocks * lanes
    window = count // 2

    def place(r):
        return (r // lanes // 2, r % lanes), r // lanes % 2

    def member(chip, core):
        return (chip[0] * 2 + core) * lanes + chip[1]

    found = {}
    for s in range(count):
        home, own_core = place(s)
        wanting = set(range(s + 1, min(count, s + window + 1)))

        def entry(chip):
            if chip == home:
                return s
            for core in (own_core, 1 - own_core):
                if member(chip, core) in wanting:
                    return member(chip, core)
            return None

        for half in (0, 1):
            for r in sorted(wanting):
                chip, _ = place(r)
                source = entry(chip)
                if source == r:
                    options = []
                    if chip[1] != home[1]:
                        options.append(entry((chip[0], home[1])))
                    if chip[0] > home[0]:
                        options.append(entry((chip[0] - 1, chip[1])))
                    if half:
                        options.reverse()
                    options = [o for o in options if o is not None] + [s]
                    source = options[0]
                found.setdefault((source - s, r - source), (set(), set()))[half].add(source)
    return sorted(found.items(), key=lambda item: (-item[0][0], item[0][1]))


def pick(me, values):
    found = jnp.int32(values[0])
    for device, value in enumerate(values):
        if value != values[0]:
            found = jnp.where(me == device, jnp.int32(value), found)
    return found


def timetable(blocks, lanes, window):
    if (blocks, lanes) == (4, 2):
        return TABLE
    return {
        "own": {step: (3,) for step in range(1, blocks * lanes)},
        "relay": {slot: ((0,), (0,)) for slot in range(1, window + 1)},
        "first": (0,),
    }


def among(me, devices):
    hit = jnp.bool_(False)
    for device in sorted(devices):
        hit = hit | (me == device)
    return hit


def kernel(
    plan, lanes, count, window, kheads,
    lengths, places_in, freq_in, keys_in, values_in, queries, out,
    places, freq, keys, values, cosine, sine, cosine_t, sine_t, kv, kfeat, qfeat, tri, qbuf, qt, scores, *rest,
):
    best, held = rest[:QUERY_PER_KEY], rest[QUERY_PER_KEY : 2 * QUERY_PER_KEY]
    q_sem, in_sem, send_sem, recv_sem = rest[2 * QUERY_PER_KEY :]
    rows = keys.shape[0]
    size = HEAD_SIZE
    group = QUERY_PER_KEY * size
    me = lax.axis_index("blk") * lanes + lax.axis_index("uly")

    def where_is(r):
        return {"blk": lax.div(r, lanes), "uly": lax.rem(r, lanes)}

    barrier = pltpu.get_barrier_semaphore()
    for offset in range(1, count):
        peer = lax.rem(me + offset, count)
        pl.semaphore_signal(
            barrier, inc=1, device_id=where_is(peer), device_id_type=pl.DeviceIdType.MESH
        )
    loads = [
        pltpu.make_async_copy(source, target, in_sem.at[i])
        for i, (source, target) in enumerate(
            ((places_in, places), (freq_in, freq), (keys_in, keys), (values_in, values))
        )
    ]
    for load in loads:
        load.start()
    fetch = pltpu.make_async_copy(queries, qbuf, q_sem)
    fetch.start()

    def column(h, width):
        return pl.ds(pl.multiple_of(h * width, width), width)

    loads[0].wait()
    loads[1].wait()
    cos_half, sin_half = rotary_tables(places[...], freq[...])
    cosine_t[...] = cos_half
    sine_t[...] = sin_half
    cosine[...] = jnp.concatenate([cos_half, cos_half], axis=0).T
    sine[...] = jnp.concatenate([-sin_half, sin_half], axis=0).T

    def turn(x):
        x = x.astype(jnp.float32)
        return (x * cosine[...] + pltpu.roll(x, size // 2, 1) * sine[...]).astype(jnp.bfloat16)

    loads[2].wait()
    loads[3].wait()

    def own_block(h, carry):
        kv[0, h, :rows, :] = turn(keys[:, column(h, size)])
        turned = values[:, column(h, size)].astype(jnp.float32).T.astype(jnp.bfloat16)
        for piece in range(rows // size):
            at = rows + piece * size
            kv[0, h, at : at + size, :] = turned[:, piece * size : (piece + 1) * size]
        return carry

    lax.fori_loop(0, kheads, own_block, 0)
    pl.semaphore_wait(barrier, count - 1)

    def copy_of(index, slot, step, h):
        return pltpu.make_async_remote_copy(
            src_ref=kv.at[slot, h],
            dst_ref=kv.at[slot + step, h],
            send_sem=send_sem.at[index, h],
            recv_sem=recv_sem.at[slot + step, h],
            device_id=where_is(me + step),
            device_id_type=pl.DeviceIdType.MESH,
        )

    def arrival(slot, h):
        return pltpu.make_async_remote_copy(
            src_ref=kv.at[slot, h],
            dst_ref=kv.at[slot, h],
            send_sem=send_sem.at[0, h],
            recv_sem=recv_sem.at[slot, h],
            device_id=where_is(me),
            device_id_type=pl.DeviceIdType.MESH,
        )

    def sends(senders, h):
        low, high = senders
        if low == high:
            return among(me, low)
        is_low = h * 2 < kheads
        return (is_low & among(me, low)) | (jnp.logical_not(is_low) & among(me, high))

    table = timetable(count // lanes, lanes, window)

    def relays(slot, h):
        hit = jnp.bool_(False)
        for (from_slot, _), senders in plan:
            if from_slot == slot:
                hit = hit | sends(senders, h)
        return hit

    def send_own(turn_at):
        for index, ((slot, step), senders) in enumerate(plan):
            if slot == 0:
                h = turn_at + pick(me, table["own"][step])

                @pl.when((h >= 0) & (h < kheads) & sends(senders, h))
                def _():
                    copy_of(index, slot, step, h).start()

    def pass_on(turn_at, place):
        for slot in sorted({slot for (slot, _), _ in plan if slot}, reverse=True):
            lead, at = table["relay"][slot]
            if place in at:
                h = turn_at + pick(me, lead)
                now = (h >= 0) & (h < kheads) & relays(slot, h)

                @pl.when(now & (pick(me, at) == place))
                def _():
                    arrival(slot, h).wait_recv()
                    for index, ((from_slot, step), senders) in enumerate(plan):
                        if from_slot == slot:
                            @pl.when(sends(senders, h))
                            def _():
                                copy_of(index, slot, step, h).start()

    def opening(i, carry):
        turn_at = i - BURST
        send_own(turn_at)
        for place in range(3):
            pass_on(turn_at, place)
        return carry

    lax.fori_loop(0, BURST - SETTLED, opening, 0)

    for slot in range(1, window + 1):
        @pl.when(me < slot)
        def _():
            def clear(h, carry):
                kv[slot, h] = jnp.zeros((rows + rows // size * size, size), kv.dtype)
                return carry

            lax.fori_loop(0, kheads, clear, 0)

    lane = lax.broadcasted_iota(jnp.int32, (1, size), 1)
    opens = jnp.zeros((1, size), jnp.int32)
    closes = jnp.zeros((1, size), jnp.int32)
    end = jnp.int32(0)
    for d in range(lengths.shape[0]):
        start, end = end, end + lengths[d]
        opens = jnp.where(lane == d, start, opens)
        closes = jnp.where(lane == d, end, closes)
    row = lax.broadcasted_iota(jnp.int32, (rows, size), 0)
    for slot in range(window + 1):
        token = row + (me - slot) * rows
        inside = (token >= opens) & (token < closes)
        kfeat[slot] = jnp.where(inside, 0.0, FAR).astype(jnp.bfloat16)
        if slot == 0:
            qfeat[...] = jnp.where(inside, 1.0, 0.0).T.astype(jnp.bfloat16)
    key_at = lax.broadcasted_iota(jnp.int32, (rows, rows), 0)
    query_at = lax.broadcasted_iota(jnp.int32, (rows, rows), 1)
    tri[...] = jnp.where(key_at <= query_at, 1.0, 0.0).astype(jnp.bfloat16)

    fetch.wait()

    def turn_queries(h, carry):
        x = qbuf[:, column(h, size)].astype(jnp.float32).T
        low, high = x[: size // 2], x[size // 2 :]
        cos_half, sin_half = cosine_t[...], sine_t[...]
        turned = jnp.concatenate(
            [low * cos_half - high * sin_half, high * cos_half + low * sin_half], axis=0
        )
        qt[h] = turned.astype(jnp.bfloat16)
        return carry

    lax.fori_loop(0, kheads * QUERY_PER_KEY, turn_queries, 0, unroll=QUERY_PER_KEY)

    scale = math.log2(math.e) / math.sqrt(size)
    ones = jnp.ones((2 * SUBLANES, rows), jnp.bfloat16)

    def key_of(slot, h):
        return jnp.concatenate([kv[slot, h, :rows, :], kfeat[slot]], axis=1)

    def value_of(slot, h):
        pieces = [
            kv[slot, h, rows + p * size : rows + (p + 1) * size, :] for p in range(rows // size)
        ]
        return jnp.concatenate([jnp.concatenate(pieces, axis=1), ones], axis=0)

    def query_of(h, g):
        return jnp.concatenate([qt[h * QUERY_PER_KEY + g], qfeat[...]], axis=0)

    def dot(a, b):
        return jnp.dot(a, b, preferred_element_type=jnp.float32)

    def begin(h):
        scores = []
        for g in range(QUERY_PER_KEY):
            q = query_of(h, g)
            scores.append(
                jnp.where(key_at <= query_at, dot(key_of(0, h), q), dot(key_of(window, h), q))
            )
        pending = None
        for g in range(QUERY_PER_KEY + 1):
            if g < QUERY_PER_KEY:
                top = jnp.max(scores[g], axis=0, keepdims=True)
                w = jnp.exp2((scores[g] - top) * scale).astype(jnp.bfloat16)
                near = w * tri[...]
                best[g][h] = jnp.broadcast_to(top, (SUBLANES, rows))
                both = dot(value_of(0, h), near) + dot(value_of(window, h), w - near)
            if pending is not None:
                held[g - 1][h] = pending[: size + SUBLANES]
            pending = both

    def complete(h):
        def score(g):
            q = query_of(h, g)
            top = best[g][h][:1]
            for slot in range(1, window):
                s = dot(key_of(slot, h), q)
                scores[g % 2, slot - 1] = s
                top = jnp.maximum(top, jnp.max(s, axis=0, keepdims=True))
            return top

        def attend(g, top):
            keep = jnp.exp2((best[g][h][:1] - top) * scale)
            both = None
            for slot in range(1, window):
                w = jnp.exp2((scores[g % 2, slot - 1] - top) * scale).astype(jnp.bfloat16)
                part = dot(value_of(slot, h), w)
                both = part if both is None else both + part
            both = both[: size + SUBLANES] + held[g][h] * keep
            settle(h, g, both)

        top = score(0)
        for g in range(QUERY_PER_KEY):
            following = score(g + 1) if g + 1 < QUERY_PER_KEY else None
            attend(g, top)
            top = following

    def settle(h, g, both):
        result = both[:size] * (1.0 / both[size : size + 1])
        at = pl.ds(pl.multiple_of(h * group + g * size, size), size)
        out[:, at] = result.T.astype(jnp.bfloat16)

    def take(slot, h):
        @pl.when((me >= slot) & jnp.logical_not(relays(slot, h)))
        def _():
            arrival(slot, h).wait_recv()

    def rounds(i, carry):
        turn_at = i - SETTLED
        send_own(turn_at)
        pass_on(turn_at, 0)
        first = turn_at + pick(me, table["first"])

        @pl.when((first >= 0) & (first < kheads))
        def _():
            take(window, first)
            begin(first)

        pass_on(turn_at, 1)

        @pl.when(turn_at >= 0)
        def _():
            for slot in range(1, window):
                take(slot, turn_at)

            @pl.when(me > 0)
            def _():
                complete(turn_at)

            @pl.when(me == 0)
            def _():
                for g in range(QUERY_PER_KEY):
                    settle(turn_at, g, held[g][turn_at])

        pass_on(turn_at, 2)
        return carry

    lax.fori_loop(0, SETTLED + kheads, rounds, 0)

    def finish(h, carry):
        for index, ((slot, step), senders) in enumerate(plan):
            @pl.when(sends(senders, h))
            def _():
                copy_of(index, slot, step, h).wait_send()

        return carry

    lax.fori_loop(0, kheads, finish, 0)


def local(blocks, lanes, queries, keys, values, positions, doc_lengths):
    rows = queries.shape[0]
    kheads = keys.shape[1] // HEAD_SIZE
    count = blocks * lanes
    window = count // 2
    plan = routes(blocks, lanes)
    vmem = pl.BlockSpec(memory_space=pltpu.VMEM)
    anywhere = pl.BlockSpec(memory_space=pl.ANY)
    freq = jnp.asarray(frequencies())
    return pl.pallas_call(
        functools.partial(kernel, plan, lanes, count, window, kheads),
        out_shape=pltpu.VMEM(queries.shape, jnp.bfloat16),
        in_specs=[pl.BlockSpec(memory_space=pltpu.SMEM)] + [anywhere] * 5,
        out_specs=vmem,
        scratch_shapes=[
            pltpu.VMEM(positions.shape, jnp.int32),
            pltpu.VMEM(freq.shape, jnp.float32),
            pltpu.VMEM(keys.shape, jnp.bfloat16),
            pltpu.VMEM(values.shape, jnp.bfloat16),
            pltpu.VMEM((rows, HEAD_SIZE), jnp.float32),
            pltpu.VMEM((rows, HEAD_SIZE), jnp.float32),
            pltpu.VMEM((HEAD_SIZE // 2, rows), jnp.float32),
            pltpu.VMEM((HEAD_SIZE // 2, rows), jnp.float32),
            pltpu.VMEM((window + 1, kheads, 2 * rows, HEAD_SIZE), jnp.bfloat16),
            pltpu.VMEM((window + 1, rows, HEAD_SIZE), jnp.bfloat16),
            pltpu.VMEM((HEAD_SIZE, rows), jnp.bfloat16),
            pltpu.VMEM((rows, rows), jnp.bfloat16),
            pltpu.VMEM(queries.shape, jnp.bfloat16),
            pltpu.VMEM((kheads * QUERY_PER_KEY, HEAD_SIZE, rows), jnp.bfloat16),
            pltpu.VMEM((2, window - 1, rows, rows), jnp.float32),
            *[pltpu.VMEM((kheads, SUBLANES, rows), jnp.float32)] * QUERY_PER_KEY,
            *[pltpu.VMEM((kheads, HEAD_SIZE + SUBLANES, rows), jnp.float32)] * QUERY_PER_KEY,
            pltpu.SemaphoreType.DMA,
            pltpu.SemaphoreType.DMA((4,)),
            pltpu.SemaphoreType.DMA((len(plan), kheads)),
            pltpu.SemaphoreType.DMA((window + 1, kheads)),
        ],
        compiler_params=pltpu.CompilerParams(
            collective_id=0, has_side_effects=True, vmem_limit_bytes=60 * 1024 * 1024
        ),
        name="windowed_attention",
    )(doc_lengths, positions, freq, keys, values, queries)


def solution(mesh):
    in_specs = (
        P(("seq", "blk", "uly"), None),
        P(("seq", "blk", "uly"), None),
        P(("seq", "blk", "uly"), None),
        P(None, ("seq", "blk", "uly")),
        P("seq"),
    )
    out_specs = P(("seq", "blk", "uly"), None)
    body = functools.partial(local, mesh.shape["blk"], mesh.shape["uly"])
    return jax.shard_map(body, mesh=mesh, in_specs=in_specs, out_specs=out_specs, check_vma=False)
```

time: 46.9 us -> 41.5 us (0.88)
  Pallas kernels: 44.9 us -> 39.8 us
    pallas_call x1, Pallas kernels: 44.9 us -> 39.8 us  [local(): pl.pallas_call(functools.partial(kernel, plan, lanes, count, window, khea...]
where the time goes in v1:
time: 41.5 us; the launch traced here: 41.3 us
  Pallas kernels  39.8 us (96%)
  local copies, waits for them, and re-layouts  1.49 us (4%)
    pallas_call x1, Pallas kernels, local(): pl.pallas_call(functools.partial(kernel, plan, lanes, count, window, khea...  39.8 us
    unnamed x1, local copies, waits for them, and re-layouts  1.49 us

profile of v1, /device:TPU:12, one launch (start us, length us, event | category | flops | bytes accessed | tf_op | source)
XLA Modules:
  0.0 41.3 jit_solution(17338941930149850996)
XLA Ops:
  0.0 39.8 %windowed_attention.1 = bf16[256,5120]{1,0:T(8,128)(2,1)S(1)} custom-call(s32[8]{0:T(128)} %lengths.1, s32[3,256]{1,0:T(4,128)} %places_in.1, f32[64,128]{1,0:T(8,128)} %constant.2.clone.freq_in, bf16[256,1024]{1,0:T(8,128)(2,1)} %keys_in.1, bf16[256,1024]{1,0:T(8,128)(2,1)} %values_in.1, bf16[256,5120]{1,0:T(8,128)(2,1)} %queries.1), custom_call_target="tpu_custom_call" | custom-call | tf_op jit(solution)/shard_map/windowed_attention/pallas_call | solution.py:435
  39.8 1.5 %copy.8 = bf16[256,5120]{1,0:T(8,128)(2,1)} copy(bf16[256,5120]{1,0:T(8,128)(2,1)S(1)} %windowed_attention.1) | data formatting | bytes 5242880

commit v2 on v1

--- a/solution.py
+++ b/solution.py
@@ -15,18 +15,40 @@
 SETTLED = 5
 FAR = -1e30
 SUBLANES = 8
+SCORES_FIRST = 5
 
 
 TABLE = {
     "own": {
-        1: (8, 4, 2, 0, 8, 8, 2, 0),
-        2: (5, 8, 0, 0, 5, 5, 0, 0),
-        4: (8, 8, 6, 3, 0, 0, 0, 0),
+        1: (
+            (8, 4, 2, 0, 8, 8, 2, 0),
+            (8, 4, 2, 0, 8, 8, 2, 0),
+            (8, 4, 2, 0, 8, 8, 2, 0),
+        ),
+        2: (
+            (5, 8, 0, 0, 5, 5, 0, 0),
+            (5, 8, 0, 0, 5, 5, 0, 0),
+            (5, 8, 0, 0, 5, 5, 0, 0),
+        ),
+        4: (
+            (8, 8, 6, 3, 0, 0, 0, 0),
+            (8, 8, 6, 3, 0, 0, 0, 0),
+            (8, 8, 6, 3, 0, 0, 0, 0),
+        ),
     },
     "relay": {
-        4: ((0, 0, 0, 0, 0, 6, 2, 2), (0, 0, 0, 0, 0, 1, 0, 0)),
-        3: ((0, 0, 0, 0, 0, 0, 1, 0), (0, 0, 0, 0, 0, 0, 2, 0)),
-        1: ((0, 0, 0, 0, 0, 2, 0, 0), (0, 1, 0, 1, 0, 1, 0, 0)),
+        4: (
+            ((0, 0, 0, 0, 0, 6, 2, 2), (0, 0, 0, 0, 0, 1, 0, 0)),
+            ((0, 0, 0, 0, 0, 6, 2, 2), (0, 0, 0, 0, 0, 1, 0, 0)),
+        ),
+        3: (
+            ((0, 0, 0, 0, 0, 0, 1, 0), (0, 0, 0, 0, 0, 0, 2, 0)),
+            ((0, 0, 0, 0, 0, 0, 1, 0), (0, 0, 0, 0, 0, 0, 2, 0)),
+        ),
+        1: (
+            ((0, 0, 0, 0, 0, 2, 0, 0), (0, 1, 0, 1, 0, 1, 0, 0)),
+            ((0, 0, 0, 0, 0, 2, 0, 0), (0, 1, 0, 1, 0, 1, 0, 0)),
+        ),
     },
     "first": (1, 2, 3, 3, 3, 4, 2, 2),
 }
@@ -121,8 +143,8 @@
     if (blocks, lanes) == (4, 2):
         return TABLE
     return {
-        "own": {step: (3,) for step in range(1, blocks * lanes)},
-        "relay": {slot: ((0,), (0,)) for slot in range(1, window + 1)},
+        "own": {step: ((3,),) * 3 for step in range(1, blocks * lanes)},
+        "relay": {slot: (((0,), (0,)),) * 2 for slot in range(1, window + 1)},
         "first": (0,),
     }
 
@@ -215,44 +237,75 @@
             device_id_type=pl.DeviceIdType.MESH,
         )
 
-    def sends(senders, h):
-        low, high = senders
-        if low == high:
-            return among(me, low)
-        is_low = h * 2 < kheads
-        return (is_low & among(me, low)) | (jnp.logical_not(is_low) & among(me, high))
-
     table = timetable(count // lanes, lanes, window)
+    half = kheads // 2
+    quarters = (0, half, kheads * 3 // 4, kheads)
+
+    def span(senders):
+        low, high = (among(me, devices) for devices in senders)
+        return jnp.where(low, 0, half), jnp.where(high, kheads, half)
+
+    spans = [span(senders) for _, senders in plan]
+    relayed = {}
+    for slot in range(1, window + 1):
+        ours = [senders for (from_slot, _), senders in plan if from_slot == slot]
+        relayed[slot] = span([set().union(*(s[part] for s in ours)) for part in (0, 1)])
 
     def relays(slot, h):
+        return (h >= relayed[slot][0]) & (h < relayed[slot][1])
+
+    own_turns = []
+    for index, ((slot, step), _) in enumerate(plan):
+        leads = table["own"][step] if slot == 0 else ()
+        edges = quarters
+        if len(set(leads)) == 1:
+            leads, edges = leads[:1], (0, kheads)
+        for part, lead in enumerate(leads):
+            ahead = pick(me, lead)
+            start = jnp.maximum(spans[index][0], edges[part]) - ahead
+            stop = jnp.minimum(spans[index][1], edges[part + 1]) - ahead
+            own_turns.append((index, step, ahead, start, stop))
+
+    relay_turns = []
+    for slot in sorted({slot for (slot, _), _ in plan if slot}, reverse=True):
+        turns, edges = table["relay"][slot], (0, half, kheads)
+        if len(set(turns)) == 1:
+            turns, edges = turns[:1], (0, kheads)
+        for part, (lead, at) in enumerate(turns):
+            ahead, where = pick(me, lead), pick(me, at)
+            start = jnp.maximum(relayed[slot][0], edges[part]) - ahead
+            stop = jnp.minimum(relayed[slot][1], edges[part + 1]) - ahead
+            for place in sorted(set(at)):
+                stop_here = jnp.where(where == place, stop, start)
+                relay_turns.append((place, slot, ahead, start, stop_here))
+
+    def due(turn_at, turns):
         hit = jnp.bool_(False)
-        for (from_slot, _), senders in plan:
-            if from_slot == slot:
-                hit = hit | sends(senders, h)
+        for *_, start, stop in turns:
+            hit = hit | ((turn_at >= start) & (turn_at < stop))
         return hit
 
     def send_own(turn_at):
-        for index, ((slot, step), senders) in enumerate(plan):
-            if slot == 0:
-                h = turn_at + pick(me, table["own"][step])
-
-                @pl.when((h >= 0) & (h < kheads) & sends(senders, h))
+        @pl.when(due(turn_at, own_turns))
+        def _():
+            for index, step, ahead, start, stop in own_turns:
+                @pl.when((turn_at >= start) & (turn_at < stop))
                 def _():
-                    copy_of(index, slot, step, h).start()
+                    copy_of(index, 0, step, turn_at + ahead).start()
 
     def pass_on(turn_at, place):
-        for slot in sorted({slot for (slot, _), _ in plan if slot}, reverse=True):
-            lead, at = table["relay"][slot]
-            if place in at:
-                h = turn_at + pick(me, lead)
-                now = (h >= 0) & (h < kheads) & relays(slot, h)
-
-                @pl.when(now & (pick(me, at) == place))
+        turns = [turn[1:] for turn in relay_turns if turn[0] == place]
+
+        @pl.when(due(turn_at, turns))
+        def _():
+            for slot, ahead, start, stop in turns:
+                @pl.when((turn_at >= start) & (turn_at < stop))
                 def _():
+                    h = turn_at + ahead
                     arrival(slot, h).wait_recv()
-                    for index, ((from_slot, step), senders) in enumerate(plan):
+                    for index, ((from_slot, step), _) in enumerate(plan):
                         if from_slot == slot:
-                            @pl.when(sends(senders, h))
+                            @pl.when((h >= spans[index][0]) & (h < spans[index][1]))
                             def _():
                                 copy_of(index, slot, step, h).start()
 
@@ -350,7 +403,7 @@
             top = best[g][h][:1]
             for slot in range(1, window):
                 s = dot(key_of(slot, h), q)
-                scores[g % 2, slot - 1] = s
+                scores[g, slot - 1] = s
                 top = jnp.maximum(top, jnp.max(s, axis=0, keepdims=True))
             return top
 
@@ -358,17 +411,21 @@
             keep = jnp.exp2((best[g][h][:1] - top) * scale)
             both = None
             for slot in range(1, window):
-                w = jnp.exp2((scores[g % 2, slot - 1] - top) * scale).astype(jnp.bfloat16)
+                w = jnp.exp2((scores[g, slot - 1] - top) * scale).astype(jnp.bfloat16)
                 part = dot(value_of(slot, h), w)
                 both = part if both is None else both + part
-            both = both[: size + SUBLANES] + held[g][h] * keep
-            settle(h, g, both)
-
-        top = score(0)
+            return both[: size + SUBLANES] + held[g][h] * keep
+
+        tops = [score(g) for g in range(SCORES_FIRST)]
+        pending = None
         for g in range(QUERY_PER_KEY):
-            following = score(g + 1) if g + 1 < QUERY_PER_KEY else None
-            attend(g, top)
-            top = following
+            if g + SCORES_FIRST < QUERY_PER_KEY:
+                tops.append(score(g + SCORES_FIRST))
+            both = attend(g, tops[g])
+            if pending is not None:
+                settle(h, g - 1, pending)
+            pending = both
+        settle(h, QUERY_PER_KEY - 1, pending)
 
     def settle(h, g, both):
         result = both[:size] * (1.0 / both[size : size + 1])
@@ -398,14 +455,7 @@
             for slot in range(1, window):
                 take(slot, turn_at)
 
-            @pl.when(me > 0)
-            def _():
-                complete(turn_at)
-
-            @pl.when(me == 0)
-            def _():
-                for g in range(QUERY_PER_KEY):
-                    settle(turn_at, g, held[g][turn_at])
+            complete(turn_at)
 
         pass_on(turn_at, 2)
         return carry
@@ -414,7 +464,7 @@
 
     def finish(h, carry):
         for index, ((slot, step), senders) in enumerate(plan):
-            @pl.when(sends(senders, h))
+            @pl.when((h >= spans[index][0]) & (h < spans[index][1]))
             def _():
                 copy_of(index, slot, step, h).wait_send()
 
@@ -452,7 +502,7 @@
             pltpu.VMEM((rows, rows), jnp.bfloat16),
             pltpu.VMEM(queries.shape, jnp.bfloat16),
             pltpu.VMEM((kheads * QUERY_PER_KEY, HEAD_SIZE, rows), jnp.bfloat16),
-            pltpu.VMEM((2, window - 1, rows, rows), jnp.float32),
+            pltpu.VMEM((QUERY_PER_KEY, window - 1, rows, rows), jnp.float32),
             *[pltpu.VMEM((kheads, SUBLANES, rows), jnp.float32)] * QUERY_PER_KEY,
             *[pltpu.VMEM((kheads, HEAD_SIZE + SUBLANES, rows), jnp.float32)] * QUERY_PER_KEY,
             pltpu.SemaphoreType.DMA,

time: 41.5 us -> 40.4 us (0.973)
  Pallas kernels: 39.8 us -> 38.7 us
    pallas_call x1, Pallas kernels: 39.8 us -> 38.7 us  [local(): pl.pallas_call(functools.partial(kernel, plan, lanes, count, window, khea...]
where the time goes in v2:
time: 40.4 us; the launch traced here: 40.2 us
  Pallas kernels  38.7 us (96%)
  local copies, waits for them, and re-layouts  1.49 us (4%)
    pallas_call x1, Pallas kernels, local(): pl.pallas_call(functools.partial(kernel, plan, lanes, count, window, khea...  38.7 us
    unnamed x1, local copies, waits for them, and re-layouts  1.49 us

profile of v2, /device:TPU:12, one launch (start us, length us, event | category | flops | bytes accessed | tf_op | source)
XLA Modules:
  0.0 40.2 jit_solution(18352358961952859657)
XLA Ops:
  0.0 38.7 %windowed_attention.1 = bf16[256,5120]{1,0:T(8,128)(2,1)S(1)} custom-call(s32[8]{0:T(128)} %lengths.1, s32[3,256]{1,0:T(4,128)} %places_in.1, f32[64,128]{1,0:T(8,128)} %constant.2.clone.freq_in, bf16[256,1024]{1,0:T(8,128)(2,1)} %keys_in.1, bf16[256,1024]{1,0:T(8,128)(2,1)} %values_in.1, bf16[256,5120]{1,0:T(8,128)(2,1)} %queries.1), custom_call_target="tpu_custom_call" | custom-call | tf_op jit(solution)/shard_map/windowed_attention/pallas_call | solution.py:485
  38.7 1.5 %copy.8 = bf16[256,5120]{1,0:T(8,128)(2,1)} copy(bf16[256,5120]{1,0:T(8,128)(2,1)S(1)} %windowed_attention.1) | data formatting | bytes 5242880

commit v3 on v2

--- a/solution.py
+++ b/solution.py
@@ -31,9 +31,9 @@
             (5, 8, 0, 0, 5, 5, 0, 0),
         ),
         4: (
-            (8, 8, 6, 3, 0, 0, 0, 0),
-            (8, 8, 6, 3, 0, 0, 0, 0),
-            (8, 8, 6, 3, 0, 0, 0, 0),
+            (8, 8, 6, 2, 0, 0, 0, 0),
+            (8, 8, 6, 2, 0, 0, 0, 0),
+            (8, 8, 6, 2, 0, 0, 0, 0),
         ),
     },
     "relay": {
@@ -462,15 +462,12 @@
 
     lax.fori_loop(0, SETTLED + kheads, rounds, 0)
 
-    def finish(h, carry):
-        for index, ((slot, step), senders) in enumerate(plan):
-            @pl.when((h >= spans[index][0]) & (h < spans[index][1]))
-            def _():
-                copy_of(index, slot, step, h).wait_send()
-
-        return carry
-
-    lax.fori_loop(0, kheads, finish, 0)
+    for index, ((slot, step), _) in enumerate(plan):
+        def finish(h, carry):
+            copy_of(index, slot, step, h).wait_send()
+            return carry
+
+        lax.fori_loop(spans[index][0], spans[index][1], finish, 0)
 
 
 def local(blocks, lanes, queries, keys, values, positions, doc_lengths):

time: 40.4 us -> 40.2 us (level)
  no operation moved by 1% of the time
where the time goes in v3:
time: 40.2 us; the launch traced here: 39.9 us
  Pallas kernels  38.4 us (96%)
  local copies, waits for them, and re-layouts  1.49 us (4%)
    pallas_call x1, Pallas kernels, local(): pl.pallas_call(functools.partial(kernel, plan, lanes, count, window, khea...  38.4 us
    unnamed x1, local copies, waits for them, and re-layouts  1.49 us

profile of v3, /device:TPU:12, one launch (start us, length us, event | category | flops | bytes accessed | tf_op | source)
XLA Modules:
  0.0 39.9 jit_solution(10300447066036926297)
XLA Ops:
  0.0 38.4 %windowed_attention.1 = bf16[256,5120]{1,0:T(8,128)(2,1)S(1)} custom-call(s32[8]{0:T(128)} %lengths.1, s32[3,256]{1,0:T(4,128)} %places_in.1, f32[64,128]{1,0:T(8,128)} %constant.2.clone.freq_in, bf16[256,1024]{1,0:T(8,128)(2,1)} %keys_in.1, bf16[256,1024]{1,0:T(8,128)(2,1)} %values_in.1, bf16[256,5120]{1,0:T(8,128)(2,1)} %queries.1), custom_call_target="tpu_custom_call" | custom-call | tf_op jit(solution)/shard_map/windowed_attention/pallas_call | solution.py:482
  38.4 1.5 %copy.8 = bf16[256,5120]{1,0:T(8,128)(2,1)} copy(bf16[256,5120]{1,0:T(8,128)(2,1)S(1)} %windowed_attention.1) | data formatting | bytes 5242880

commit v4 on v3

--- a/solution.py
+++ b/solution.py
@@ -349,16 +349,18 @@
     fetch.wait()
 
     def turn_queries(h, carry):
-        x = qbuf[:, column(h, size)].astype(jnp.float32).T
-        low, high = x[: size // 2], x[size // 2 :]
         cos_half, sin_half = cosine_t[...], sine_t[...]
-        turned = jnp.concatenate(
-            [low * cos_half - high * sin_half, high * cos_half + low * sin_half], axis=0
-        )
-        qt[h] = turned.astype(jnp.bfloat16)
+        x = qbuf[:, column(h, group)].T
+        for g in range(QUERY_PER_KEY):
+            low = x[g * size : g * size + size // 2].astype(jnp.float32)
+            high = x[g * size + size // 2 : (g + 1) * size].astype(jnp.float32)
+            turned = jnp.concatenate(
+                [low * cos_half - high * sin_half, high * cos_half + low * sin_half], axis=0
+            )
+            qt[h * QUERY_PER_KEY + g] = turned.astype(jnp.bfloat16)
         return carry
 
-    lax.fori_loop(0, kheads * QUERY_PER_KEY, turn_queries, 0, unroll=QUERY_PER_KEY)
+    lax.fori_loop(0, kheads, turn_queries, 0)
 
     scale = math.log2(math.e) / math.sqrt(size)
     ones = jnp.ones((2 * SUBLANES, rows), jnp.bfloat16)

time: 40.2 us -> 40.3 us (level)
  no operation moved by 1% of the time
where the time goes in v4:
time: 40.3 us; the launch traced here: 40.1 us
  Pallas kernels  38.6 us (96%)
  local copies, waits for them, and re-layouts  1.49 us (4%)
    pallas_call x1, Pallas kernels, local(): pl.pallas_call(functools.partial(kernel, plan, lanes, count, window, khea...  38.6 us
    unnamed x1, local copies, waits for them, and re-layouts  1.49 us

profile of v4, /device:TPU:12, one launch (start us, length us, event | category | flops | bytes accessed | tf_op | source)
XLA Modules:
  0.0 40.1 jit_solution(8175983740939685033)
XLA Ops:
  0.0 38.6 %windowed_attention.1 = bf16[256,5120]{1,0:T(8,128)(2,1)S(1)} custom-call(s32[8]{0:T(128)} %lengths.1, s32[3,256]{1,0:T(4,128)} %places_in.1, f32[64,128]{1,0:T(8,128)} %constant.2.clone.freq_in, bf16[256,1024]{1,0:T(8,128)(2,1)} %keys_in.1, bf16[256,1024]{1,0:T(8,128)(2,1)} %values_in.1, bf16[256,5120]{1,0:T(8,128)(2,1)} %queries.1), custom_call_target="tpu_custom_call" | custom-call | tf_op jit(solution)/shard_map/windowed_attention/pallas_call | solution.py:484
  38.6 1.5 %copy.8 = bf16[256,5120]{1,0:T(8,128)(2,1)} copy(bf16[256,5120]{1,0:T(8,128)(2,1)S(1)} %windowed_attention.1) | data formatting | bytes 5242880
